TPU v7x, 32 devices: a whole 2x2x4 slice. The times are simulated.
32 devices in a mesh: dp: 4 (over y, core), vocab: 8 (over z, x).
Axes of the slice: x: 2, y: 2, z: 4, core: 2. Of those that a mesh axis runs over, the one named last changes fastest.
Arguments:
- student_hidden: bfloat16 [512, 2048], P('dp', 'vocab'), may hold values from -210 to 210
- student_blocks: bfloat16 [8, 1024, 4864], P('vocab', 'dp'), may hold values from -0.375 to 0.375
- teacher_logits: bfloat16 [512, 19456], P('dp', 'vocab'), may hold values from -16 to 308
- token_ids: int32 [512], P('dp'), may hold values from 0 to 19455
- loss_mask: int32 [512], P('dp'), may hold values from 0 to 1, as said below
Outputs:
- hidden_grad: bfloat16 [512, 2048], P('dp', 'vocab')
- token_kl: float32 [512], P('dp')
- sampled_logprob: float32 [512], P('dp')
- loss: float32 [], replicated
Inputs may be any that keep to these rules, and one draw needn't show every extreme that they name: `loss_mask`: in each block of 128 tokens the mask is 0 on a leading run of at most 64 tokens and 1 on the rest.
All inputs are finite; a program needn't handle non-finite values.
Results may differ from a plain program's by a relative error of at most 0.0047.
Values may be sent and summed in bfloat16 or wider, within the bound.
No kernel may reach another device: no remote copies, remote signals or barrier semaphores. Data moves between devices by JAX's collectives and lax.ppermute only.
A program may use at most 64 MiB of HBM per device.

v0:
```python
import jax
import jax.numpy as jnp
from jax import lax
from jax.sharding import PartitionSpec as P

D = 2048
VT = 2432


def swapped(shard, axis, stride):
    return lax.ppermute(shard, axis, [(i, i ^ 1 << stride) for i in range(lax.axis_size(axis))])


def combined_all(part, axis, combine):
    gathered = jax.tree.map(lambda a: lax.all_gather(a, axis), part)

    def take(source):
        return jax.tree.map(lambda a: lax.dynamic_index_in_dim(a, source, 0, False), gathered)

    return lax.fori_loop(
        1, lax.axis_size(axis), lambda source, state: combine(state, take(source)), take(0)
    )


def pair_merge(left_pair, right_pair):
    left_max, left_total = left_pair
    right_max, right_total = right_pair
    top_value = jnp.maximum(left_max, right_max)
    merged_total = left_total * jnp.exp(left_max - top_value) + right_total * jnp.exp(
        right_max - top_value
    )
    return (top_value, merged_total)


def row_stats(values):
    row_max = jnp.max(values, axis=1)
    row_total = jnp.sum(jnp.exp(values - row_max[:, None]), axis=1)
    return (row_max, row_total)


def on_device(student_hidden, student_blocks, teacher_logits, token_ids, loss_mask):
    vocab_index = lax.axis_index("vocab")
    pair_side = vocab_index % 2
    mask_float = loss_mask.astype(jnp.float32)
    mask_total = lax.psum(jnp.sum(mask_float), "dp")
    gathered = lax.all_gather(student_hidden, "vocab", axis=1, tiled=True)
    piece = student_blocks[0]
    own_block = lax.dynamic_slice_in_dim(piece, pair_side * VT, VT, 1)
    far_block = lax.dynamic_slice_in_dim(piece, (1 - pair_side) * VT, VT, 1)
    received = swapped(far_block, "vocab", 0)
    stacked = jnp.where(
        pair_side == 0, jnp.stack([own_block, received]), jnp.stack([received, own_block])
    )
    weight = lax.all_gather(stacked, "dp", axis=1, tiled=True).reshape(D, VT)
    logits = jnp.dot(gathered, weight, preferred_element_type=jnp.float32)
    column_start = vocab_index * VT
    teacher_local = teacher_logits.astype(jnp.float32)
    teacher_full = teacher_logits.astype(jnp.float32)
    teacher_max = lax.pmax(jnp.max(teacher_full, axis=1), "vocab")
    teacher_total = lax.psum(jnp.sum(jnp.exp(teacher_full - teacher_max[:, None]), axis=1), "vocab")
    student_max, student_total = row_stats(logits)
    merged = combined_all((student_max, student_total), "vocab", pair_merge)
    stats = (teacher_max, teacher_total, merged[0], merged[1])
    teacher_logp = teacher_local - stats[0][:, None] - jnp.log(stats[1])[:, None]
    student_logp = logits - stats[2][:, None] - jnp.log(stats[3])[:, None]
    teacher_prob = jnp.exp(teacher_logp)
    kl_part = jnp.sum(teacher_prob * (teacher_logp - student_logp), axis=1)
    columns = lax.broadcasted_iota(jnp.int32, logits.shape, 1) + column_start
    sampled_part = jnp.sum(jnp.where(columns == token_ids[:, None], student_logp, 0.0), axis=1)
    token_kl, sampled = lax.psum((kl_part, sampled_part), "vocab")
    loss = lax.psum(jnp.sum(mask_float * token_kl), "dp") / mask_total
    factor = mask_float / mask_total
    dlogits = (factor[:, None] * (jnp.exp(student_logp) - teacher_prob)).astype(jnp.bfloat16)
    term = lax.dot_general(
        dlogits, weight, (((1,), (1,)), ((), ())), preferred_element_type=jnp.float32
    )
    hidden_grad = lax.psum_scatter(term, "vocab", scatter_dimension=1, tiled=True).astype(
        jnp.bfloat16
    )
    return (hidden_grad, token_kl, sampled, loss)


def solution(mesh):
    return jax.shard_map(
        on_device,
        mesh=mesh,
        in_specs=(P("dp", "vocab"), P("vocab", "dp", None), P("dp", "vocab"), P("dp"), P("dp")),
        out_specs=(P("dp", "vocab"), P("dp"), P("dp"), P()),
        check_vma=False,
    )
```

profile of v0, /device:TPU:0, one launch (start us, length us, event | category | flops | bytes accessed | tf_op | source)
XLA Modules:
  0.0 265.2 jit_solution(2844016320098941567)
XLA Ops:
  7.2 0.0 all-gather.6.cloned.1.call-start
  7.2 2.9 %constant_dynamic-slice_fusion.1 = (bf16[1,256,2432]{2,1,0:T(8,128)(2,1)S(1)}, bf16[256,2432]{1,0:T(8,128)(2,1)}) fusion(bf16[1,256,4864]{2,1,0:T(8,128)(2,1)} %param.8, s32[]{:T(128)S(6)} %select_n.41, s32[]{:T(128)S(6)} %select_n.42), kind=kLoop, calls=%fused_computation.33 | loop fusion | bytes 4980744 | tf_op jit(solution)/shard_map/dynamic_slice | solution.py:48
  10.1 3.0 %collective-permute-start = (bf16[256,2432]{1,0:T(8,128)(2,1)}, bf16[256,2432]{1,0:T(8,128)(2,1)S(1)}, u32[]{:S(2)}, u32[]{:S(2)}) collective-permute-start(bf16[256,2432]{1,0:T(8,128)(2,1)} %get-tuple-element.160), channel_id=1, source_target_pairs={{0,1},{1,0},{2,3},{3,2},{4,5},{5,4},{6,7},{7,6},{8,9},{9,8},{10,11... | collective-permute-start | bytes 3735560 | tf_op jit(solution)/shard_map/ppermute | solution.py:11
  13.1 27.6 %collective-permute-done = bf16[256,2432]{1,0:T(8,128)(2,1)S(1)} collective-permute-done((bf16[256,2432]{1,0:T(8,128)(2,1)}, bf16[256,2432]{1,0:T(8,128)(2,1)S(1)}, u32[]{:S(2)}, u32[]{:S(2)}) %collective-permute-start) | collective-permute-done | bytes 1245216 | tf_op jit(solution)/shard_map/ppermute | solution.py:11
  40.7 1.8 maximum_select_fusion
  42.5 0.0 copy-start
  42.5 0.0 all-gather.6.cloned.1.call-update
  42.5 0.0 reduce-scatter.2.cloned.1.call-start
  42.6 1.0 copy-done
  43.6 0.0 copy-start.1
  43.6 0.3 copy.10
  43.9 0.2 reduce_max.24
  44.1 21.9 %pmax.7 = f32[128]{0:T(128)S(1)} all-reduce(bf16[128]{0:T(256)(128)(2,1)S(1)} %reduce_max.24), channel_id=1, replica_groups=mesh['dp'=4,'vocab'=8] {'vocab'}, use_global_device_ids=true, to_apply=%region_7.8 | all-reduce | flops 128 | bytes 768 | tf_op jit(solution)/shard_map/pmax | solution.py:59
  66.0 0.3 exponential_reduce_fusion
  66.3 17.1 %psum.36 = f32[128]{0:T(128)S(1)} all-reduce(f32[128]{0:T(128)S(1)} %exponential_reduce_fusion), channel_id=1, replica_groups=mesh['dp'=4,'vocab'=8] {'vocab'}, use_global_device_ids=true, to_apply=%region_9.10 | all-reduce | flops 128 | bytes 1024 | tf_op jit(solution)/shard_map/psum | solution.py:60
  83.5 0.0 copy-done.1
  83.5 31.2 %all_gather.19 = bf16[128,2048]{1,0:T(8,128)(2,1)S(1)} all-gather(bf16[128,256]{1,0:T(8,128)(2,1)S(1)} %copy-done.1), channel_id=1, replica_groups=mesh['dp'=4,'vocab'=8] {'vocab'}, dimensions={1}, use_global_device_ids=true | all-gather | bytes 589824 | tf_op jit(solution)/shard_map/all_gather | solution.py:46
  114.7 0.0 all-gather.6.cloned.1.call-done
  114.7 6.6 %fusion.17 = (f32[128]{0:T(128)S(1)}, f32[2432,128]{1,0:T(8,128)S(1)}) fusion(bf16[2048,2432]{1,0:T(8,128)(2,1)} %bitcast.46, bf16[128,2048]{1,0:T(8,128)(2,1)S(1)} %all_gather.19), kind=kOutput, calls=%fused_computation.36 | convolution fusion | flops 1275379584 | bytes 11731456 | tf_op jit(solution)/shard_map/dot_general | solution.py:55
  121.4 0.0 copy-start.2
  121.4 0.3 exponential_reduce_fusion.1
  121.7 0.0 copy-start.3
  121.7 18.5 %all-gather.3 = f32[8,1,128]{2,1,0:T(1,128)S(1)} all-gather(f32[1,1,128]{2,1,0:T(1,128)S(1)} %bitcast.52), channel_id=3, replica_groups=mesh['dp'=4,'vocab'=8] {'vocab'}, dimensions={0}, use_global_device_ids=true | all-gather | bytes 4608 | tf_op jit(solution)/shard_map/all_gather | solution.py:15
  140.2 16.3 %all-gather.2 = f32[8,1,128]{2,1,0:T(1,128)S(1)} all-gather(f32[1,1,128]{2,1,0:T(1,128)S(1)} %bitcast.51), channel_id=2, replica_groups=mesh['dp'=4,'vocab'=8] {'vocab'}, dimensions={0}, use_global_device_ids=true | all-gather | bytes 4608 | tf_op jit(solution)/shard_map/all_gather | solution.py:15
  156.5 0.3 while.17
  156.8 0.0 copy-done.2
  156.8 1.1 fusion.7
  157.9 19.7 %all-reduce = (f32[128]{0:T(128)S(1)}, f32[128]{0:T(128)}) all-reduce(f32[128]{0:T(128)S(1)} %get-tuple-element.140, f32[128]{0:T(128)S(1)} %get-tuple-element.139), channel_id=1, replica_groups=mesh['dp'=4,'vocab'=8] {'vocab'}, use_global_device_ids=true, to_apply=%region_12.13 | all-reduce | flops 256 | bytes 2048 | tf_op jit(solution)/shard_map/psum | solution.py:70
  177.6 0.0 copy-start.4
  177.6 0.0 copy-done.3
  177.6 0.6 multiply_reduce_fusion
  178.2 6.3 %all-reduce.1 = (f32[]{:T(128)}, f32[]{:T(128)}) all-reduce(f32[]{:T(128)} %get-tuple-element.142, f32[]{:T(128)} %get-tuple-element.141), channel_id=1, replica_groups=mesh['dp'=4,'vocab'=8] {'dp'}, use_global_device_ids=true, to_apply=%region_1.2 | all-reduce | flops 2 | bytes 16 | tf_op jit(solution)/shard_map/psum | solution.py:45
  184.4 0.6 convert_divide_fusion
  185.1 8.2 %fusion.10 = f32[128,2048]{1,0:T(8,128)} fusion(bf16[2048,2432]{1,0:T(8,128)(2,1)} %bitcast.47, bf16[128,2432]{0,1:T(8,128)(2,1)S(1)} %copy.10, f32[2432,128]{1,0:T(8,128)S(1)} %get-tuple-element.162, f32[128]{0:T(128)S(1)} %log.7, f32[128]{0:T(128)S(1)} %pmax.7, f32[128]{0:T(128)S(1)} %log.6, f32[128]{0:T(128)S(1)} %get-tuple-element.137, ...), kind=kOutput, calls=%fused_computation.23 | convolution fusion | flops 1277558784 | bytes 12880384 | tf_op jit(solution)/shard_map/dot_general | solution.py:74
  193.3 0.0 copy-done.4
  193.3 0.0 reduce-scatter.2.cloned.1.call-update
  194.7 61.0 %reduce-scatter.2.cloned.1.call-done = f32[128,256]{1,0:T(8,128)} async-done(((f32[128,2048]{1,0:T(8,128)}), f32[128,256]{1,0:T(8,128)}) %reduce-scatter.2.cloned.1.call-update) | async-done | bytes 131088 | tf_op jit(solution)/shard_map/reduce_scatter | solution.py:77
  255.7 1.5 convert_element_type.16
  (12 shorter events, 0.2 us)
Async XLA Ops:
  7.2 107.5 %all-gather.6.cloned.1.call-start = ((), (), s32[]{:S(2)}) async-start(), calls=%async_computation.1 | async-start | bytes 12451840 | tf_op jit(solution)/shard_map/all_gather | solution.py:54
  10.1 30.5 %collective-permute-start = (bf16[256,2432]{1,0:T(8,128)(2,1)}, bf16[256,2432]{1,0:T(8,128)(2,1)S(1)}, u32[]{:S(2)}, u32[]{:S(2)}) collective-permute-start(bf16[256,2432]{1,0:T(8,128)(2,1)} %get-tuple-element.160), channel_id=1, source_target_pairs={{0,1},{1,0},{2,3},{3,2},{4,5},{5,4},{6,7},{7,6},{8,9},{9,8},{10,11... | collective-permute-start | bytes 3735560 | tf_op jit(solution)/shard_map/ppermute | solution.py:11
  42.5 1.1 copy-start
  42.5 213.1 %reduce-scatter.2.cloned.1.call-start = ((), (), s32[]{:S(2)}) async-start(), calls=%async_computation.2 | async-start | bytes 1179648 | tf_op jit(solution)/shard_map/reduce_scatter | solution.py:77
  43.6 39.9 %copy-start.1 = (bf16[128,256]{1,0:T(8,128)(2,1)S(1)}, bf16[128,256]{1,0:T(8,128)(2,1)}, u32[]{:S(2)}) copy-start(bf16[128,256]{1,0:T(8,128)(2,1)} %param.7) | copy-start | bytes 196612
  121.4 35.4 %copy-start.2 = (s32[128]{0:T(128)S(1)}, s32[128]{0:T(128)}, u32[]{:S(2)}) copy-start(s32[128]{0:T(128)} %param.10) | copy-start | bytes 1540
  121.7 55.9 %copy-start.3 = (s32[128]{0:T(128)S(1)}, s32[128]{0:T(128)}, u32[]{:S(2)}) copy-start(s32[128]{0:T(128)} %param.11) | copy-start | bytes 1540
  177.6 15.8 %copy-start.4 = (f32[128]{0:T(128)}, f32[128]{0:T(128)S(1)}, u32[]{:S(2)}) copy-start(f32[128]{0:T(128)S(1)} %get-tuple-element.153) | copy-start | bytes 1540
Sparse Core Ops, SparseCore 0:
  42.6 68.6 all-gather.5
  193.5 62.1 reduce-scatter.1
where the time goes:
time: 266 us; the launch traced here: 265 us
  blocking collectives  131 us (49%)
  waiting for transfers between devices  88.6 us (33%)
  between operations  16.6 us (6%)
  matrix products  14.9 us (6%)
  other arithmetic  6.81 us (3%)
  local copies, waits for them, and re-layouts  4.23 us (2%)
  starting transfers between devices  3.05 us (1%)
    reduce_scatter x1, waiting for transfers between devices, on_device(): lax.psum_scatter(term, 'vocab', scatter_dimension=1, tiled=True)  61 us
    all_gather x2, blocking collectives, combined_all(): gathered = jax.tree.map(lambda a: lax.all_gather(a, axis), part)  34.7 us
    all_gather x1, blocking collectives, on_device(): gathered = lax.all_gather(student_hidden, 'vocab', axis=1, tiled=True)  31.2 us
    ppermute x1, waiting for transfers between devices, swapped(): lax.ppermute(shard, axis, [(i, i ^ 1 << stride) for i in range(lax.axis_s...  27.6 us
    pmax x1, blocking collectives, on_device(): teacher_max = lax.pmax(jnp.max(teacher_full, axis=1), 'vocab')  21.9 us
    psum x1, blocking collectives, on_device(): token_kl, sampled = lax.psum((kl_part, sampled_part), 'vocab')  19.7 us
    psum x1, blocking collectives, on_device(): lax.psum(jnp.sum(jnp.exp(teacher_full - teacher_max[:, None]), axis=1), '...  17.1 us
    dot_general x1, matrix products, on_device(): lax.dot_general(dlogits, weight, (((1,), (1,)), ((), ())), preferred_elem...  8.22 us
  transfers between devices with their start and end apart: 3, of which 2 were waited for; matrix products, arithmetic and copies ran while one was open for 0% of the time, Pallas kernels for 0%

commit v1 on v0

--- a/solution.py
+++ b/solution.py
@@ -43,7 +43,7 @@
     pair_side = vocab_index % 2
     mask_float = loss_mask.astype(jnp.float32)
     mask_total = lax.psum(jnp.sum(mask_float), "dp")
-    gathered = lax.all_gather(student_hidden, "vocab", axis=1, tiled=True)
+    gathered = jnp.concatenate(lax.all_gather(student_hidden, "vocab"), axis=1)
     piece = student_blocks[0]
     own_block = lax.dynamic_slice_in_dim(piece, pair_side * VT, VT, 1)
     far_block = lax.dynamic_slice_in_dim(piece, (1 - pair_side) * VT, VT, 1)

time: 266 us -> 266 us (level)
  no operation moved by 1% of the time
where the time goes in v1:
time: 266 us; the launch traced here: 265 us
  blocking collectives  131 us (49%)
  waiting for transfers between devices  88.6 us (33%)
  between operations  16.6 us (6%)
  matrix products  14.9 us (6%)
  other arithmetic  6.81 us (3%)
  local copies, waits for them, and re-layouts  4.26 us (2%)
  starting transfers between devices  3.05 us (1%)
    reduce_scatter x1, waiting for transfers between devices, on_device(): lax.psum_scatter(term, 'vocab', scatter_dimension=1, tiled=True)  61 us
    all_gather x2, blocking collectives, combined_all(): gathered = jax.tree.map(lambda a: lax.all_gather(a, axis), part)  34.7 us
    all_gather x1, blocking collectives, on_device(): gathered = jnp.concatenate(lax.all_gather(student_hidden, 'vocab'), axis=1)  32 us
    ppermute x1, waiting for transfers between devices, swapped(): lax.ppermute(shard, axis, [(i, i ^ 1 << stride) for i in range(lax.axis_s...  27.6 us
    pmax x1, blocking collectives, on_device(): teacher_max = lax.pmax(jnp.max(teacher_full, axis=1), 'vocab')  21.2 us
    psum x1, blocking collectives, on_device(): token_kl, sampled = lax.psum((kl_part, sampled_part), 'vocab')  19.6 us
    psum x1, blocking collectives, on_device(): lax.psum(jnp.sum(jnp.exp(teacher_full - teacher_max[:, None]), axis=1), '...  17.1 us
    dot_general x1, matrix products, on_device(): lax.dot_general(dlogits, weight, (((1,), (1,)), ((), ())), preferred_elem...  8.22 us
  transfers between devices with their start and end apart: 3, of which 2 were waited for; matrix products, arithmetic and copies ran while one was open for 0% of the time, Pallas kernels for 0%

profile of v1, /device:TPU:0, one launch (start us, length us, event | category | flops | bytes accessed | tf_op | source)
XLA Modules:
  0.0 265.2 jit_solution(5867003953455832097)
XLA Ops:
  7.2 0.0 all-gather.7.cloned.1.call-start
  7.2 2.9 %constant_dynamic-slice_fusion.1 = (bf16[1,256,2432]{2,1,0:T(8,128)(2,1)S(1)}, bf16[256,2432]{1,0:T(8,128)(2,1)}) fusion(bf16[1,256,4864]{2,1,0:T(8,128)(2,1)} %param.8, s32[]{:T(128)S(6)} %select_n.41, s32[]{:T(128)S(6)} %select_n.42), kind=kLoop, calls=%fused_computation.33 | loop fusion | bytes 4980744 | tf_op jit(solution)/shard_map/dynamic_slice | solution.py:48
  10.1 3.0 %collective-permute-start = (bf16[256,2432]{1,0:T(8,128)(2,1)}, bf16[256,2432]{1,0:T(8,128)(2,1)S(1)}, u32[]{:S(2)}, u32[]{:S(2)}) collective-permute-start(bf16[256,2432]{1,0:T(8,128)(2,1)} %get-tuple-element.160), channel_id=1, source_target_pairs={{0,1},{1,0},{2,3},{3,2},{4,5},{5,4},{6,7},{7,6},{8,9},{9,8},{10,11... | collective-permute-start | bytes 3735560 | tf_op jit(solution)/shard_map/ppermute | solution.py:11
  13.1 27.6 %collective-permute-done = bf16[256,2432]{1,0:T(8,128)(2,1)S(1)} collective-permute-done((bf16[256,2432]{1,0:T(8,128)(2,1)}, bf16[256,2432]{1,0:T(8,128)(2,1)S(1)}, u32[]{:S(2)}, u32[]{:S(2)}) %collective-permute-start) | collective-permute-done | bytes 1245216 | tf_op jit(solution)/shard_map/ppermute | solution.py:11
  40.7 1.8 maximum_select_fusion
  42.5 0.0 copy-start.1
  42.5 0.0 all-gather.7.cloned.1.call-update
  42.5 0.0 copy-start
  42.5 0.0 reduce-scatter.2.cloned.1.call-start
  42.6 0.8 copy-done.1
  43.3 32.0 %all-gather = bf16[1024,256]{1,0:T(8,128)(2,1)S(1)} all-gather(bf16[128,256]{1,0:T(8,128)(2,1)S(1)} %copy-done.1), channel_id=2, replica_groups=mesh['dp'=4,'vocab'=8] {'vocab'}, dimensions={0}, use_global_device_ids=true | all-gather | bytes 589824 | tf_op jit(solution)/shard_map/all_gather | solution.py:46
  75.3 0.3 copy.13
  75.6 0.0 copy-done
  75.6 0.3 copy.14
  75.9 0.2 reduce_max.24
  76.1 21.2 %pmax.7 = f32[128]{0:T(128)S(1)} all-reduce(bf16[128]{0:T(256)(128)(2,1)S(1)} %reduce_max.24), channel_id=1, replica_groups=mesh['dp'=4,'vocab'=8] {'vocab'}, use_global_device_ids=true, to_apply=%region_7.8 | all-reduce | flops 128 | bytes 768 | tf_op jit(solution)/shard_map/pmax | solution.py:59
  97.3 0.3 exponential_reduce_fusion
  97.6 17.1 %psum.36 = f32[128]{0:T(128)S(1)} all-reduce(f32[128]{0:T(128)S(1)} %exponential_reduce_fusion), channel_id=1, replica_groups=mesh['dp'=4,'vocab'=8] {'vocab'}, use_global_device_ids=true, to_apply=%region_9.10 | all-reduce | flops 128 | bytes 1024 | tf_op jit(solution)/shard_map/psum | solution.py:60
  114.8 0.0 all-gather.7.cloned.1.call-done
  114.8 6.6 %fusion.17 = (f32[128]{0:T(128)S(1)}, f32[2432,128]{1,0:T(8,128)S(1)}) fusion(bf16[2048,2432]{1,0:T(8,128)(2,1)} %bitcast.50, bf16[128,2048]{0,1:T(8,128)(2,1)S(1)} %bitcast.54), kind=kOutput, calls=%fused_computation.36 | convolution fusion | flops 1275379584 | bytes 11731456 | tf_op jit(solution)/shard_map/dot_general | solution.py:55
  121.4 0.0 copy-start.2
  121.4 0.3 exponential_reduce_fusion.1
  121.8 0.0 copy-start.3
  121.8 18.4 %all-gather.4 = f32[8,1,128]{2,1,0:T(1,128)S(1)} all-gather(f32[1,1,128]{2,1,0:T(1,128)S(1)} %bitcast.58), channel_id=4, replica_groups=mesh['dp'=4,'vocab'=8] {'vocab'}, dimensions={0}, use_global_device_ids=true | all-gather | bytes 4608 | tf_op jit(solution)/shard_map/all_gather | solution.py:15
  140.2 16.3 %all-gather.3 = f32[8,1,128]{2,1,0:T(1,128)S(1)} all-gather(f32[1,1,128]{2,1,0:T(1,128)S(1)} %bitcast.57), channel_id=3, replica_groups=mesh['dp'=4,'vocab'=8] {'vocab'}, dimensions={0}, use_global_device_ids=true | all-gather | bytes 4608 | tf_op jit(solution)/shard_map/all_gather | solution.py:15
  156.5 0.3 while.17
  156.8 0.0 copy-done.2
  156.8 1.1 fusion.7
  157.9 19.6 %all-reduce = (f32[128]{0:T(128)S(1)}, f32[128]{0:T(128)}) all-reduce(f32[128]{0:T(128)S(1)} %get-tuple-element.140, f32[128]{0:T(128)S(1)} %get-tuple-element.139), channel_id=1, replica_groups=mesh['dp'=4,'vocab'=8] {'vocab'}, use_global_device_ids=true, to_apply=%region_12.13 | all-reduce | flops 256 | bytes 2048 | tf_op jit(solution)/shard_map/psum | solution.py:70
  177.6 0.0 copy-start.4
  177.6 0.0 copy-done.3
  177.6 0.6 multiply_reduce_fusion
  178.2 6.3 %all-reduce.1 = (f32[]{:T(128)}, f32[]{:T(128)}) all-reduce(f32[]{:T(128)} %get-tuple-element.142, f32[]{:T(128)} %get-tuple-element.141), channel_id=1, replica_groups=mesh['dp'=4,'vocab'=8] {'dp'}, use_global_device_ids=true, to_apply=%region_1.2 | all-reduce | flops 2 | bytes 16 | tf_op jit(solution)/shard_map/psum | solution.py:45
  184.4 0.6 convert_divide_fusion
  185.1 8.2 %fusion.10 = f32[128,2048]{1,0:T(8,128)} fusion(bf16[2048,2432]{1,0:T(8,128)(2,1)} %bitcast.51, bf16[128,2432]{0,1:T(8,128)(2,1)S(1)} %copy.14, f32[2432,128]{1,0:T(8,128)S(1)} %get-tuple-element.162, f32[128]{0:T(128)S(1)} %log.7, f32[128]{0:T(128)S(1)} %pmax.7, f32[128]{0:T(128)S(1)} %log.6, f32[128]{0:T(128)S(1)} %get-tuple-element.137, ...), kind=kOutput, calls=%fused_computation.23 | convolution fusion | flops 1277558784 | bytes 12880384 | tf_op jit(solution)/shard_map/dot_general | solution.py:74
  193.3 0.0 copy-done.4
  193.3 0.0 reduce-scatter.2.cloned.1.call-update
  194.7 61.0 %reduce-scatter.2.cloned.1.call-done = f32[128,256]{1,0:T(8,128)} async-done(((f32[128,2048]{1,0:T(8,128)}), f32[128,256]{1,0:T(8,128)}) %reduce-scatter.2.cloned.1.call-update) | async-done | bytes 131088 | tf_op jit(solution)/shard_map/reduce_scatter | solution.py:77
  255.7 1.5 convert_element_type.16
  (12 shorter events, 0.2 us)
Async XLA Ops:
  7.2 107.6 %all-gather.7.cloned.1.call-start = ((), (), s32[]{:S(2)}) async-start(), calls=%async_computation.1 | async-start | bytes 12451840 | tf_op jit(solution)/shard_map/all_gather | solution.py:54
  10.1 30.5 %collective-permute-start = (bf16[256,2432]{1,0:T(8,128)(2,1)}, bf16[256,2432]{1,0:T(8,128)(2,1)S(1)}, u32[]{:S(2)}, u32[]{:S(2)}) collective-permute-start(bf16[256,2432]{1,0:T(8,128)(2,1)} %get-tuple-element.160), channel_id=1, source_target_pairs={{0,1},{1,0},{2,3},{3,2},{4,5},{5,4},{6,7},{7,6},{8,9},{9,8},{10,11... | collective-permute-start | bytes 3735560 | tf_op jit(solution)/shard_map/ppermute | solution.py:11
  42.5 0.8 copy-start.1
  42.5 33.1 %copy-start = (bf16[128,2432]{1,0:T(8,128)(2,1)S(1)}, bf16[128,2432]{1,0:T(8,128)(2,1)}, u32[]{:S(2)}) copy-start(bf16[128,2432]{1,0:T(8,128)(2,1)} %param.9) | copy-start | bytes 1867780
  42.5 213.2 %reduce-scatter.2.cloned.1.call-start = ((), (), s32[]{:S(2)}) async-start(), calls=%async_computation.2 | async-start | bytes 1179648 | tf_op jit(solution)/shard_map/reduce_scatter | solution.py:77
  121.4 35.3 %copy-start.2 = (s32[128]{0:T(128)S(1)}, s32[128]{0:T(128)}, u32[]{:S(2)}) copy-start(s32[128]{0:T(128)} %param.10) | copy-start | bytes 1540
  121.8 55.8 %copy-start.3 = (s32[128]{0:T(128)S(1)}, s32[128]{0:T(128)}, u32[]{:S(2)}) copy-start(s32[128]{0:T(128)} %param.11) | copy-start | bytes 1540
  177.6 15.8 %copy-start.4 = (f32[128]{0:T(128)}, f32[128]{0:T(128)S(1)}, u32[]{:S(2)}) copy-start(f32[128]{0:T(128)S(1)} %get-tuple-element.153) | copy-start | bytes 1540
Sparse Core Ops, SparseCore 0:
  42.6 68.6 all-gather.6
  193.5 62.1 reduce-scatter.1
